TPU v7x, 32 devices: a whole 2x2x4 slice. The times are simulated.
32 devices in a mesh: dp: 2 (over x), expert: 16 (over z, y, core).
Axes of the slice: x: 2, y: 2, z: 4, core: 2. Of those that a mesh axis runs over, the one named last changes fastest.
Arguments:
- gradients: bfloat16 [16, 1024, 5888], P(None, ('dp', 'expert')), may hold values from -6 to 6
- momentum: bfloat16 [16, 1024, 5888], P('expert', 'dp'), may hold values from -6 to 6
- right_factor: bfloat16 [16, 5888, 256], P('expert', 'dp'), may hold values from -6 to 6
Outputs:
- new_momentum: bfloat16 [16, 1024, 5888], P('expert', 'dp')
- new_factor: bfloat16 [16, 5888, 256], P('expert', 'dp')
- update_rows: bfloat16 [16, 1024, 5888], P(None, ('dp', 'expert'))
All inputs are finite; a program needn't handle non-finite values.
Results may differ from a plain program's by a relative error of at most 0.009.
Values may be sent and summed in bfloat16 or wider, within the bound.
A program may use at most 128 MiB of HBM per device.

v0:
```python
import math

import jax
import jax.numpy as jnp
from jax import lax
from jax.sharding import PartitionSpec as P

D = 5888
FFW = 1024
RANK = 256


decay_rate = 0.95
epsilon = 1e-06


def body(gradients, momentum, right_factor):
    arrived = lax.all_to_all(gradients, "expert", split_axis=0, concat_axis=1, tiled=True)
    rank_cols = right_factor.shape[2]
    blended = (
        decay_rate * momentum[0].astype(jnp.float32) + arrived[0].astype(jnp.float32)
    ).astype(jnp.bfloat16)
    columns = blended
    left = jnp.dot(
        columns,
        lax.all_gather(right_factor[0], "dp", axis=0, tiled=True),
        preferred_element_type=jnp.float32,
    )
    gram_matrix = lax.psum(jnp.dot(left.T, left, precision=lax.Precision.HIGHEST), "dp")
    lower = jnp.linalg.cholesky(gram_matrix)
    inverse = jax.scipy.linalg.solve_triangular(
        lower, jnp.eye(rank_cols, dtype=jnp.float32), lower=True
    )
    ortho = jnp.dot(left, inverse.T, precision=lax.Precision.HIGHEST).astype(jnp.bfloat16)
    columns = blended
    right_half = lax.psum_scatter(
        lax.dot_general(
            columns, ortho, (((0,), (0,)), ((), ())), preferred_element_type=jnp.float32
        ),
        "dp",
        scatter_dimension=0,
        tiled=True,
    )
    column = lax.psum(jnp.sum(right_half * right_half, axis=0), "dp")
    own_factor = (right_half * lax.rsqrt(column / D + epsilon)).astype(jnp.bfloat16)
    right_rounded = lax.all_gather(right_half.astype(jnp.bfloat16), "dp", axis=0, tiled=True)
    full_factor = lax.all_gather(own_factor, "dp", axis=0, tiled=True)
    kept = (
        blended.astype(jnp.float32)
        - (1.0 - decay_rate)
        * lax.dot_general(
            ortho, right_rounded, (((1,), (1,)), ((), ())), preferred_element_type=jnp.float32
        )
    ).astype(jnp.bfloat16)
    update = (
        math.sqrt(FFW / RANK)
        * lax.dot_general(
            ortho, full_factor, (((1,), (1,)), ((), ())), preferred_element_type=jnp.float32
        )
    ).astype(jnp.bfloat16)
    moments = [kept]
    factors = [own_factor]
    updates = [update]
    returned = lax.all_to_all(jnp.stack(updates), "expert", split_axis=1, concat_axis=0, tiled=True)
    return (jnp.stack(moments), jnp.stack(factors), returned)


def solution(mesh):
    in_specs = (P(None, ("dp", "expert"), None), P("expert", "dp", None), P("expert", "dp", None))
    out_specs = (P("expert", "dp", None), P("expert", "dp", None), P(None, ("dp", "expert"), None))
    return jax.shard_map(body, mesh=mesh, in_specs=in_specs, out_specs=out_specs, check_vma=False)
```

profile of v0, /device:TPU:13, one launch (start us, length us, event | category | flops | bytes accessed | tf_op | source)
XLA Modules:
  0.0 616.2 jit_solution(494227464245584876)
XLA Ops:
  7.2 6.5 %all-to-all-start = ((bf16[16,32,5888]{2,1,0:T(8,128)(2,1)}), bf16[16,32,5888]{2,1,0:T(8,128)(2,1)}, u32[]{:S(2)}, u32[]{:S(2)}) async-start(bf16[16,32,5888]{2,1,0:T(8,128)(2,1)} %param.3), calls=%async_computation | async-start | bytes 12058624 | tf_op jit(solution)/shard_map/all_to_all | solution.py:18
  14.5 131.0 %all-to-all-done = bf16[16,32,5888]{2,1,0:T(8,128)(2,1)} async-done(((bf16[16,32,5888]{2,1,0:T(8,128)(2,1)}), bf16[16,32,5888]{2,1,0:T(8,128)(2,1)}, u32[]{:S(2)}, u32[]{:S(2)}) %all-to-all-start) | async-done | bytes 6029344 | tf_op jit(solution)/shard_map/all_to_all | solution.py:18
  145.5 8.9 %fusion = bf16[512,5888]{1,0:T(8,128)(2,1)} fusion(bf16[1,512,5888]{2,1,0:T(8,128)(2,1)} %param.4, bf16[16,32,5888]{2,1,0:T(8,128)(2,1)} %all-to-all-done), kind=kLoop, calls=%fused_computation.3 | loop fusion | flops 15073280 | bytes 18087936 | tf_op jit(solution)/shard_map/convert_element_type | solution.py:22
  154.3 5.3 fusion.3
  159.7 1.7 fusion.18
  161.7 22.1 %all-reduce.3.cloned.1.call-done = f32[256,256]{0,1:T(8,128)} async-done(((f32[256,256]{0,1:T(8,128)}), f32[256,256]{0,1:T(8,128)}) %all-reduce.3.cloned.1.call-update) | async-done | bytes 262160 | tf_op jit(solution)/shard_map/psum | solution.py:29
  183.8 1.1 copy.12
  184.8 1.0 fusion.8
  185.8 11.7 %cholesky.50 = f32[128,128]{1,0:T(8,128)S(1)} custom-call(f32[128,128]{1,0:T(8,128)S(1)} %cholesky.118), custom_call_target="Cholesky" | custom-call | tf_op jit(solution)/shard_map/jit(cholesky)/cholesky | solution.py:30
  197.6 9.8 %custom-call.15 = f32[1,128,128]{1,2,0:T(8,128)S(1)} custom-call(f32[1,128,128]{2,1,0:T(8,128)S(1)} %get-tuple-element.26), custom_call_target="InvertDiagBlocksLowerTriangular" | custom-call | tf_op jit(solution)/shard_map/jit(cholesky)/cholesky | solution.py:30
  207.9 11.7 %cholesky.105 = f32[128,128]{1,0:T(8,128)S(1)} custom-call(f32[128,128]{1,0:T(8,128)S(1)} %convolution_subtract_fusion.1), custom_call_target="Cholesky" | custom-call | tf_op jit(solution)/shard_map/jit(cholesky)/cholesky | solution.py:30
  219.7 0.7 compare_reduce_fusion
  221.8 4.3 while.1
  222.6 1.4 bitcast_dynamic-update-slice_fusion.2
  224.7 1.4 bitcast_dynamic-update-slice_fusion.2
  226.1 19.7 %custom-call.16 = f32[2,128,128]{1,2,0:T(8,128)S(1)} custom-call(f32[2,128,128]{2,1,0:T(8,128)S(1)} %get-tuple-element.10), custom_call_target="InvertDiagBlocksLowerTriangular" | custom-call | tf_op jit(solution)/shard_map/jit(_solve_triangular)/triangular_solve | solution.py:31
  247.3 7.1 %fusion.19 = f32[5888,256]{1,0:T(8,128)} fusion(bf16[512,5888]{1,0:T(8,128)(2,1)} %fusion, bf16[512,256]{1,0:T(8,128)(2,1)S(1)} %convolution_convert_fusion), kind=kOutput, calls=%fused_computation.47 | convolution fusion | flops 1543503872 | bytes 12320768 | tf_op jit(solution)/shard_map/dot_general | solution.py:37
  254.5 74.7 %reduce-scatter.2.cloned.1.call-done = f32[2944,256]{1,0:T(8,128)} async-done(((f32[5888,256]{1,0:T(8,128)}), f32[2944,256]{1,0:T(8,128)}) %reduce-scatter.2.cloned.1.call-update) | async-done | bytes 3014672 | tf_op jit(solution)/shard_map/reduce_scatter | solution.py:36
  329.2 2.3 multiply_reduce_fusion
  331.5 3.8 psum.15
  335.2 4.8 multiply_convert_fusion.1
  340.0 44.8 %all-gather.7.cloned.1.call-done = bf16[5888,256]{1,0:T(8,128)(2,1)} async-done(((bf16[2944,256]{1,0:T(8,128)(2,1)}), bf16[5888,256]{1,0:T(8,128)(2,1)}) %all-gather.7.cloned.1.call-update) | async-done | bytes 3014672 | tf_op jit(solution)/shard_map/all_gather | solution.py:47
  384.8 3.6 fusion.2
  388.4 10.8 %copy.17 = bf16[1,512,5888]{2,0,1:T(2,128)(2,1)} copy(bf16[1,512,5888]{2,1,0:T(8,128)(2,1)S(1)} %fusion.2) | data formatting | bytes 12058624 | tf_op jit(solution)/shard_map/stack | solution.py:64
  399.8 38.3 %reduce.12 = bf16[512,5888]{1,0:T(8,128)(2,1)} reduce(bf16[512,1,5888]{2,1,0:T(2,128)(2,1)} %bitcast.60, bf16[]{:T(256)} %broadcast.118), dimensions={1}, to_apply=%bitcast.52.reduce_sub_computation | reduce | bytes 12058626
  438.1 11.3 %reshape.59 = bf16[16,2,94208]{2,1,0:T(2,128)(2,1)} reshape(bf16[512,5888]{1,0:T(8,128)(2,1)} %reduce.12) | data formatting | bytes 12058624
  449.5 6.5 %all-to-all-start.1 = ((bf16[16,2,94208]{2,1,0:T(2,128)(2,1)}), bf16[16,2,94208]{2,1,0:T(2,128)(2,1)}, u32[]{:S(2)}, u32[]{:S(2)}) async-start(bf16[16,2,94208]{2,1,0:T(2,128)(2,1)} %reshape.59), calls=%async_computation.2 | async-start | bytes 12058624 | tf_op jit(solution)/shard_map/all_to_all | solution.py:64
  456.6 44.4 %all-gather.5.cloned.1.call-done = bf16[5888,256]{1,0:T(8,128)(2,1)} async-done(((bf16[2944,256]{1,0:T(8,128)(2,1)}), bf16[5888,256]{1,0:T(8,128)(2,1)}) %all-gather.5.cloned.1.call-update) | async-done | bytes 3014672 | tf_op jit(solution)/shard_map/all_gather | solution.py:46
  501.0 8.0 %fusion.1 = bf16[1,512,5888]{2,1,0:T(8,128)(2,1)} fusion(bf16[512,256]{1,0:T(8,128)(2,1)S(1)} %convolution_convert_fusion, bf16[5888,256]{1,0:T(8,128)(2,1)} %all-gather.5.cloned.1.call-done, bf16[512,5888]{1,0:T(8,128)(2,1)} %fusion), kind=kOutput, calls=%fused_computation.6 | convolution fusion | flops 1555562496 | bytes 15335424 | tf_op jit(solution)/shard_map/dot_general | solution.py:51
  509.0 78.8 %all-to-all-done.1 = bf16[16,2,94208]{2,1,0:T(2,128)(2,1)} async-done(((bf16[16,2,94208]{2,1,0:T(2,128)(2,1)}), bf16[16,2,94208]{2,1,0:T(2,128)(2,1)}, u32[]{:S(2)}, u32[]{:S(2)}) %all-to-all-start.1) | async-done | bytes 6029344 | tf_op jit(solution)/shard_map/all_to_all | solution.py:64
  587.8 14.0 %reshape.60 = bf16[512,1,5888]{2,1,0:T(2,128)(2,1)} reshape(bf16[16,2,94208]{2,1,0:T(2,128)(2,1)} %all-to-all-done.1) | data formatting | bytes 12058624
  601.8 7.9 %copy.15 = bf16[1,512,5888]{2,1,0:T(8,128)(2,1)} copy(bf16[1,512,5888]{2,0,1:T(2,128)(2,1)} %bitcast.59) | data formatting | bytes 12058624
  (32 shorter events, 5.6 us)
Async XLA Ops:
  7.2 138.3 %all-to-all-start = ((bf16[16,32,5888]{2,1,0:T(8,128)(2,1)}), bf16[16,32,5888]{2,1,0:T(8,128)(2,1)}, u32[]{:S(2)}, u32[]{:S(2)}) async-start(bf16[16,32,5888]{2,1,0:T(8,128)(2,1)} %param.3), calls=%async_computation | async-start | bytes 12058624 | tf_op jit(solution)/shard_map/all_to_all | solution.py:18
  13.7 140.6 %all-gather.9.cloned.1.call-start = ((), (), s32[]{:S(2)}) async-start(), calls=%async_computation.7 | async-start | bytes 4521984 | tf_op jit(solution)/shard_map/all_gather | solution.py:26
  14.4 169.3 %all-reduce.3.cloned.1.call-start = ((), (), s32[]{:S(2)}) async-start(), calls=%async_computation.3 | async-start | bytes 524288 | tf_op jit(solution)/shard_map/psum | solution.py:29
  161.4 167.8 %reduce-scatter.2.cloned.1.call-start = ((), (), s32[]{:S(2)}) async-start(), calls=%async_computation.4 | async-start | bytes 9043968 | tf_op jit(solution)/shard_map/reduce_scatter | solution.py:36
  254.4 130.4 %all-gather.7.cloned.1.call-start = ((), (), s32[]{:S(2)}) async-start(), calls=%async_computation.6 | async-start | bytes 4521984 | tf_op jit(solution)/shard_map/all_gather | solution.py:47
  449.5 138.3 %all-to-all-start.1 = ((bf16[16,2,94208]{2,1,0:T(2,128)(2,1)}), bf16[16,2,94208]{2,1,0:T(2,128)(2,1)}, u32[]{:S(2)}, u32[]{:S(2)}) async-start(bf16[16,2,94208]{2,1,0:T(2,128)(2,1)} %reshape.59), calls=%async_computation.2 | async-start | bytes 12058624 | tf_op jit(solution)/shard_map/all_to_all | solution.py:64
  456.0 45.0 %all-gather.5.cloned.1.call-start = ((), (), s32[]{:S(2)}) async-start(), calls=%async_computation.5 | async-start | bytes 4521984 | tf_op jit(solution)/shard_map/all_gather | solution.py:46
Sparse Core Ops, SparseCore 0:
  16.0 43.8 all-gather.8
  161.5 22.1 all-reduce.2
  254.5 74.6 reduce-scatter.1
  340.2 44.5 all-gather.6
  458.0 42.9 all-gather.4
where the time goes:
time: 617 us; the launch traced here: 616 us
  waiting for transfers between devices  397 us (64%)
  other arithmetic  109 us (18%)
  local copies, waits for them, and re-layouts  49.9 us (8%)
  matrix products  27.7 us (4%)
  between operations  15.3 us (2%)
  starting transfers between devices  13.7 us (2%)
    all_to_all x1, waiting for transfers between devices, body(): lax.all_to_all(gradients, 'expert', split_axis=0, concat_axis=1, tiled=True)  131 us
    all_to_all x1, waiting for transfers between devices, body(): lax.all_to_all(jnp.stack(updates), 'expert', split_axis=1, concat_axis=0,...  78.8 us
    reduce_scatter x1, waiting for transfers between devices, body(): lax.psum_scatter(lax.dot_general(columns, ortho, (((0,), (0,)), ((), ()))...  74.7 us
    all_gather x1, waiting for transfers between devices, body(): full_factor = lax.all_gather(own_factor, 'dp', axis=0, tiled=True)  44.8 us
    all_gather x1, waiting for transfers between devices, body(): lax.all_gather(right_half.astype(jnp.bfloat16), 'dp', axis=0, tiled=True)  44.4 us
    unnamed x2, other arithmetic  38.3 us
    another operation x6, other arithmetic, body(): lower = jnp.linalg.cholesky(gram_matrix)  34 us
    unnamed x4, local copies, waits for them, and re-layouts  33.8 us
  transfers between devices with their start and end apart: 7, of which 6 were waited for; matrix products, arithmetic and copies ran while one was open for 3% of the time, Pallas kernels for 0%

commit v1 on v0

v1 whole, which is shorter than its diff:
```python
import math

import jax
import jax.numpy as jnp
from jax import lax
from jax.sharding import PartitionSpec as P

decay_rate = 0.95
epsilon = 1e-06
CHUNKS = 2


def make_body(dp):
    def others(value, wire=None):
        sent = value if wire is None else value.astype(wire)
        for step in range(1, dp):
            yield step, lax.ppermute(sent, "dp", [(i, (i + step) % dp) for i in range(dp)])

    def body(gradients, momentum, right_factor):
        place = lax.axis_index("dp")
        experts = gradients.shape[0]
        rows, width = momentum.shape[1], momentum.shape[2]
        depth, rank = right_factor.shape[1], right_factor.shape[2]
        factor = jnp.zeros((dp * depth, rank), right_factor.dtype)
        factor = lax.dynamic_update_slice(factor, right_factor[0], (place * depth, 0))
        for step, block in others(right_factor[0]):
            factor = lax.dynamic_update_slice(factor, block, ((place - step) % dp * depth, 0))
        arrived = lax.all_to_all(gradients, "expert", split_axis=0, concat_axis=0, tiled=True)
        arrived = arrived.reshape(rows, width)
        blended = (
            decay_rate * momentum[0].astype(jnp.float32) + arrived.astype(jnp.float32)
        ).astype(jnp.bfloat16)
        left = jnp.dot(blended, factor, preferred_element_type=jnp.float32)
        gram = jnp.dot(left.T, left, precision=lax.Precision.HIGHEST)
        gram_matrix = gram
        for _, block in others(gram):
            gram_matrix = gram_matrix + block
        lower = jnp.linalg.cholesky(gram_matrix)
        inverse = jax.scipy.linalg.solve_triangular(
            lower, jnp.eye(rank, dtype=jnp.float32), lower=True
        )
        ortho = jnp.dot(left, inverse.T, precision=lax.Precision.HIGHEST).astype(jnp.bfloat16)
        pieces = CHUNKS if width % (128 * CHUNKS) == 0 else 1
        size = width // pieces
        rights = []
        for k in range(pieces):
            part = lax.dot_general(
                blended[:, k * size : (k + 1) * size],
                ortho,
                (((0,), (0,)), ((), ())),
                preferred_element_type=jnp.float32,
            )
            total = part
            for _, block in others(part, jnp.bfloat16):
                total = total + block.astype(jnp.float32)
            rights.append(total)
        right = jnp.concatenate(rights, axis=0)
        column = jnp.sum(right * right, axis=0)
        new_factor = (right * lax.rsqrt(column / width + epsilon)).astype(jnp.bfloat16)
        update = (
            math.sqrt(rows * dp / rank)
            * lax.dot_general(
                ortho, new_factor, (((1,), (1,)), ((), ())), preferred_element_type=jnp.float32
            )
        ).astype(jnp.bfloat16)
        returned = lax.all_to_all(
            update.reshape(experts, rows // experts, width),
            "expert",
            split_axis=0,
            concat_axis=0,
            tiled=True,
        )
        kept = (
            blended.astype(jnp.float32)
            - (1.0 - decay_rate)
            * lax.dot_general(
                ortho,
                right.astype(jnp.bfloat16),
                (((1,), (1,)), ((), ())),
                preferred_element_type=jnp.float32,
            )
        ).astype(jnp.bfloat16)
        own_factor = lax.dynamic_slice(new_factor, (place * depth, 0), (depth, rank))
        return kept[None], own_factor[None], returned

    return body


def solution(mesh):
    in_specs = (P(None, ("dp", "expert"), None), P("expert", "dp", None), P("expert", "dp", None))
    out_specs = (P("expert", "dp", None), P("expert", "dp", None), P(None, ("dp", "expert"), None))
    return jax.shard_map(
        make_body(mesh.shape["dp"]),
        mesh=mesh,
        in_specs=in_specs,
        out_specs=out_specs,
        check_vma=False,
    )
```

time: 617 us -> 442 us (0.72)
  waiting for transfers between devices: 397 us -> 318 us
  other arithmetic: 109 us -> 62.1 us
  local copies, waits for them, and re-layouts: 49.9 us -> 17.7 us
  between operations: 15.3 us -> 2.15 us
    ppermute x0 -> x4, waiting for transfers between devices: none -> 99.6 us  [others(): lax.ppermute(sent, 'dp', [(i, (i + step) % dp) for i in range(dp)])]
    all_gather x3 -> x0, waiting for transfers between devices: 89.2 us -> none  [the longest x1 44.8 us: body(): full_factor = lax.all_gather(own_factor, 'dp', axis=0, tiled=True)]
    reduce_scatter x1 -> x0, waiting for transfers between devices: 74.7 us -> none  [body(): lax.psum_scatter(lax.dot_general(columns, ortho, (((0,), (0,)), ((), ()))...]
    unnamed x2, other arithmetic: 38.3 us -> 0.01 us
    unnamed x4 -> x15, local copies, waits for them, and re-layouts: 33.8 us -> 6.56 us
    psum x1 -> x0, waiting for transfers between devices: 22.1 us -> none  [body(): lax.psum(jnp.dot(left.T, left, precision=lax.Precision.HIGHEST), 'dp')]
    another operation x8 -> x7, local copies, waits for them, and re-layouts: 15 us -> 4 us  [the longest x1 10.8 us: body(): jnp.stack(updates)]
    all_to_all x2, waiting for transfers between devices: 210 us -> 219 us  [the longest x1 122 us: body(): lax.all_to_all(update.reshape(experts, rows // experts, width), 'expert',...]
  transfers between devices with their start and end apart: 7 -> 6, of which waited for: 6 -> 6; matrix products, arithmetic and copies ran while one was open for 3% -> 3% of each run, Pallas kernels for 0% -> 0%
where the time goes in v1:
time: 442 us; the launch traced here: 441 us
  waiting for transfers between devices  318 us (72%)
  other arithmetic  62.1 us (14%)
  matrix products  23.9 us (5%)
  local copies, waits for them, and re-layouts  17.7 us (4%)
  starting transfers between devices  17.3 us (4%)
    all_to_all x1, waiting for transfers between devices, body(): lax.all_to_all(update.reshape(experts, rows // experts, width), 'expert',...  122 us
    ppermute x4, waiting for transfers between devices, others(): lax.ppermute(sent, 'dp', [(i, (i + step) % dp) for i in range(dp)])  99.6 us
    all_to_all x1, waiting for transfers between devices, body(): lax.all_to_all(gradients, 'expert', split_axis=0, concat_axis=0, tiled=True)  96.2 us
    another operation x6, other arithmetic, body(): lower = jnp.linalg.cholesky(gram_matrix)  34.1 us
    another operation x3, other arithmetic, body(): jax.scipy.linalg.solve_triangular(lower, jnp.eye(rank, dtype=jnp.float32)...  19.7 us
  transfers between devices with their start and end apart: 6, of which 6 were waited for; matrix products, arithmetic and copies ran while one was open for 3% of the time, Pallas kernels for 0%

profile of v1, /device:TPU:13, one launch (start us, length us, event | category | flops | bytes accessed | tf_op | source)
XLA Modules:
  0.0 441.3 jit_solution(3154252429844775047)
XLA Ops:
  0.6 6.7 %all-to-all-start = ((bf16[16,32,5888]{2,1,0:T(8,128)(2,1)}), bf16[16,32,5888]{2,1,0:T(8,128)(2,1)}, u32[]{:S(2)}, u32[]{:S(2)}) async-start(bf16[16,32,5888]{2,1,0:T(8,128)(2,1)} %param.3), calls=%async_computation | async-start | bytes 12058624 | tf_op jit(solution)/shard_map/all_to_all | solution.py:28
  7.3 1.3 collective-permute-start
  8.6 1.8 broadcast_in_dim.12
  10.4 1.2 constant_dynamic-update-slice_fusion.2
  11.6 30.0 %collective-permute-done = bf16[2944,256]{1,0:T(8,128)(2,1)S(1)} collective-permute-done((bf16[2944,256]{1,0:T(8,128)(2,1)S(1)}, bf16[2944,256]{1,0:T(8,128)(2,1)S(1)}, u32[]{:S(2)}, u32[]{:S(2)}) %collective-permute-start) | collective-permute-done | bytes 1507360 | tf_op jit(solution)/shard_map/ppermute | solution.py:17
  41.6 1.2 constant_dynamic-update-slice_fusion.1
  42.9 96.2 %all-to-all-done = bf16[16,32,5888]{2,1,0:T(8,128)(2,1)} async-done(((bf16[16,32,5888]{2,1,0:T(8,128)(2,1)}), bf16[16,32,5888]{2,1,0:T(8,128)(2,1)}, u32[]{:S(2)}, u32[]{:S(2)}) %all-to-all-start) | async-done | bytes 6029344 | tf_op jit(solution)/shard_map/all_to_all | solution.py:28
  139.1 6.2 %fusion = bf16[512,5888]{1,0:T(8,128)(2,1)S(1)} fusion(bf16[1,512,5888]{2,1,0:T(8,128)(2,1)} %param.4, bf16[16,32,5888]{2,1,0:T(8,128)(2,1)} %all-to-all-done), kind=kLoop, calls=%fused_computation.3 | loop fusion | flops 15073280 | bytes 18087936 | tf_op jit(solution)/shard_map/convert_element_type | solution.py:32
  145.4 5.8 %fusion.24 = f32[512,256]{1,0:T(8,128)S(1)} fusion(bf16[512,5888]{1,0:T(8,128)(2,1)S(1)} %fusion, bf16[5888,256]{1,0:T(8,128)(2,1)} %constant_dynamic-update-slice_fusion.1), kind=kOutput, calls=%fused_computation.56 | convolution fusion | flops 1543503872 | bytes 9568256 | tf_op jit(solution)/shard_map/dot_general | solution.py:33
  151.1 1.0 fusion.25
  152.2 1.3 collective-permute-start.1
  153.5 6.5 %collective-permute-done.1 = f32[256,256]{0,1:T(8,128)S(1)} collective-permute-done((f32[256,256]{0,1:T(8,128)S(1)}, f32[256,256]{0,1:T(8,128)S(1)}, u32[]{:S(2)}, u32[]{:S(2)}) %collective-permute-start.1) | collective-permute-done | bytes 262176 | tf_op jit(solution)/shard_map/ppermute | solution.py:17
  160.2 11.7 %cholesky.50 = f32[128,128]{1,0:T(8,128)S(1)} custom-call(f32[128,128]{1,0:T(8,128)S(1)} %cholesky.118), custom_call_target="Cholesky" | custom-call | tf_op jit(solution)/shard_map/jit(cholesky)/cholesky | solution.py:38
  171.9 9.8 %custom-call.15 = f32[1,128,128]{1,2,0:T(8,128)S(1)} custom-call(f32[1,128,128]{2,1,0:T(8,128)S(1)} %get-tuple-element.24), custom_call_target="InvertDiagBlocksLowerTriangular" | custom-call | tf_op jit(solution)/shard_map/jit(cholesky)/cholesky | solution.py:38
  182.3 11.9 %cholesky.105 = f32[128,128]{1,0:T(8,128)S(1)} custom-call(f32[128,128]{1,0:T(8,128)S(1)} %slice_subtract_fusion), custom_call_target="Cholesky" | custom-call | tf_op jit(solution)/shard_map/jit(cholesky)/cholesky | solution.py:38
  196.3 4.0 while.1
  196.9 1.4 bitcast_dynamic-update-slice_fusion.2
  198.8 1.4 bitcast_dynamic-update-slice_fusion.2
  200.2 19.7 %custom-call.16 = f32[2,128,128]{1,2,0:T(8,128)S(1)} custom-call(f32[2,128,128]{2,1,0:T(8,128)S(1)} %get-tuple-element.10), custom_call_target="InvertDiagBlocksLowerTriangular" | custom-call | tf_op jit(solution)/shard_map/jit(_solve_triangular)/triangular_solve | solution.py:39
  221.4 3.2 fusion.22
  224.6 1.3 collective-permute-start.3
  225.9 1.0 fusion.23
  227.2 31.0 %collective-permute-done.3 = bf16[2944,256]{1,0:T(8,128)(2,1)S(1)} collective-permute-done((bf16[2944,256]{1,0:T(8,128)(2,1)S(1)}, bf16[2944,256]{1,0:T(8,128)(2,1)S(1)}, u32[]{:S(2)}, u32[]{:S(2)}) %collective-permute-start.3) | collective-permute-done | bytes 1507360 | tf_op jit(solution)/shard_map/ppermute | solution.py:17
  258.5 32.0 %collective-permute-done.2 = bf16[2944,256]{1,0:T(8,128)(2,1)S(1)} collective-permute-done((bf16[2944,256]{1,0:T(8,128)(2,1)S(1)}, bf16[2944,256]{1,0:T(8,128)(2,1)S(1)}, u32[]{:S(2)}, u32[]{:S(2)}) %collective-permute-start.2) | collective-permute-done | bytes 1507360 | tf_op jit(solution)/shard_map/ppermute | solution.py:17
  290.8 0.8 multiply_reduce_fusion
  291.6 0.8 copy-done.1
  293.0 4.3 multiply_convert_fusion
  297.3 6.5 %all-to-all-start.1 = ((bf16[16,32,5888]{2,1,0:T(8,128)(2,1)}), bf16[16,32,5888]{2,1,0:T(8,128)(2,1)}, u32[]{:S(2)}, u32[]{:S(2)}) async-start(bf16[16,32,5888]{2,1,0:T(8,128)(2,1)} %bitcast.55), calls=%async_computation.1 | async-start | bytes 12058624 | tf_op jit(solution)/shard_map/all_to_all | solution.py:66
  303.8 2.8 dynamic-slice_bitcast_fusion
  306.6 6.7 %fusion.1 = bf16[1,512,5888]{2,1,0:T(8,128)(2,1)} fusion(bf16[512,256]{1,0:T(8,128)(2,1)S(1)} %convolution_convert_fusion, bf16[512,5888]{1,0:T(8,128)(2,1)} %copy-done, f32[2944,256]{1,0:T(8,128)S(1)} %convert_add_fusion.1, f32[2944,256]{1,0:T(8,128)S(1)} %copy-done.2), kind=kOutput, calls=%fused_computation.6 | convolution fusion | flops 1561591808 | bytes 18350080 | tf_op jit(solution)/shard_map/dot_general | solution.py:76
  313.3 122.3 %all-to-all-done.1 = bf16[16,32,5888]{2,1,0:T(8,128)(2,1)} async-done(((bf16[16,32,5888]{2,1,0:T(8,128)(2,1)}), bf16[16,32,5888]{2,1,0:T(8,128)(2,1)}, u32[]{:S(2)}, u32[]{:S(2)}) %all-to-all-start.1) | async-done | bytes 6029344 | tf_op jit(solution)/shard_map/all_to_all | solution.py:66
  435.6 5.7 %copy.25 = bf16[16,32,5888]{2,1,0:T(8,128)(2,1)} copy(bf16[16,32,5888]{2,1,0:T(8,128)(2,1)} %all-to-all-done.1) | data formatting | bytes 12058624
  (42 shorter events, 5.6 us)
Async XLA Ops:
  0.6 6.7 %copy-start.4 = (bf16[1,2944,256]{2,1,0:T(8,128)(2,1)S(1)}, bf16[1,2944,256]{2,1,0:T(8,128)(2,1)}, u32[]{:S(2)}) copy-start(bf16[1,2944,256]{2,1,0:T(8,128)(2,1)} %param.5) | copy-start | bytes 4521988
  0.6 138.5 %all-to-all-start = ((bf16[16,32,5888]{2,1,0:T(8,128)(2,1)}), bf16[16,32,5888]{2,1,0:T(8,128)(2,1)}, u32[]{:S(2)}, u32[]{:S(2)}) async-start(bf16[16,32,5888]{2,1,0:T(8,128)(2,1)} %param.3), calls=%async_computation | async-start | bytes 12058624 | tf_op jit(solution)/shard_map/all_to_all | solution.py:28
  7.3 34.3 %collective-permute-start = (bf16[2944,256]{1,0:T(8,128)(2,1)S(1)}, bf16[2944,256]{1,0:T(8,128)(2,1)S(1)}, u32[]{:S(2)}, u32[]{:S(2)}) collective-permute-start(bf16[2944,256]{1,0:T(8,128)(2,1)S(1)} %bitcast.56), channel_id=1, source_target_pairs={{0,16},{16,0},{1,17},{17,1},{2,18},{18,2},{3,19},{19,3},{4,20},{20... | collective-permute-start | bytes 4521992 | tf_op jit(solution)/shard_map/ppermute | solution.py:17
  145.3 5.8 %copy-start = (bf16[512,5888]{1,0:T(8,128)(2,1)}, bf16[512,5888]{1,0:T(8,128)(2,1)S(1)}, u32[]{:S(2)}) copy-start(bf16[512,5888]{1,0:T(8,128)(2,1)S(1)} %fusion) | copy-start | bytes 18087940
  152.2 7.8 %collective-permute-start.1 = (f32[256,256]{0,1:T(8,128)S(1)}, f32[256,256]{0,1:T(8,128)S(1)}, u32[]{:S(2)}, u32[]{:S(2)}) collective-permute-start(f32[256,256]{0,1:T(8,128)S(1)} %fusion.25), channel_id=1, source_target_pairs={{0,16},{16,0},{1,17},{17,1},{2,18},{18,2},{3,19},{19,3},{4,20},{20... | collective-permute-start | bytes 786440 | tf_op jit(solution)/shard_map/ppermute | solution.py:17
  220.8 5.1 %slice-start = ((s8[6029312]{0:T(1024)(128)(4,1)}), s8[4194304]{0:T(1024)(128)(4,1)S(1)}, s32[]{:S(2)}) async-start(s8[6029312]{0:T(1024)(128)(4,1)} %bitcast.53), calls=%async_computation.2 | async-start | bytes 8388608
  221.4 4.5 %slice-start.1 = ((s8[6029312]{0:T(1024)(128)(4,1)}), s8[1835008]{0:T(1024)(128)(4,1)S(1)}, s32[]{:S(2)}) async-start(s8[6029312]{0:T(1024)(128)(4,1)} %bitcast.53), calls=%async_computation.3 | async-start | bytes 3670016
  224.6 33.6 %collective-permute-start.3 = (bf16[2944,256]{1,0:T(8,128)(2,1)S(1)}, bf16[2944,256]{1,0:T(8,128)(2,1)S(1)}, u32[]{:S(2)}, u32[]{:S(2)}) collective-permute-start(bf16[2944,256]{1,0:T(8,128)(2,1)S(1)} %get-tuple-element.27), channel_id=1, source_target_pairs={{0,16},{16,0},{1,17},{17,1},{2,18},{18,2},{3,19},{19,3},{4,20},{20... | collective-permute-start | bytes 4521992 | tf_op jit(solution)/shard_map/ppermute | solution.py:17
  226.9 63.7 %collective-permute-start.2 = (bf16[2944,256]{1,0:T(8,128)(2,1)S(1)}, bf16[2944,256]{1,0:T(8,128)(2,1)S(1)}, u32[]{:S(2)}, u32[]{:S(2)}) collective-permute-start(bf16[2944,256]{1,0:T(8,128)(2,1)S(1)} %get-tuple-element.29), channel_id=1, source_target_pairs={{0,16},{16,0},{1,17},{17,1},{2,18},{18,2},{3,19},{19,3},{4,20},{20... | collective-permute-start | bytes 4521992 | tf_op jit(solution)/shard_map/ppermute | solution.py:17
  290.8 1.6 copy-start.1
  292.9 4.4 copy-start.3
  297.3 138.3 %all-to-all-start.1 = ((bf16[16,32,5888]{2,1,0:T(8,128)(2,1)}), bf16[16,32,5888]{2,1,0:T(8,128)(2,1)}, u32[]{:S(2)}, u32[]{:S(2)}) async-start(bf16[16,32,5888]{2,1,0:T(8,128)(2,1)} %bitcast.55), calls=%async_computation.1 | async-start | bytes 12058624 | tf_op jit(solution)/shard_map/all_to_all | solution.py:66
  303.8 2.8 copy-start.2

commit v2 on v1

--- a/solution.py
+++ b/solution.py
@@ -1,16 +1,139 @@
+import functools
 import math
 
 import jax
 import jax.numpy as jnp
 from jax import lax
+from jax.experimental import pallas as pl
+from jax.experimental.pallas import tpu as pltpu
 from jax.sharding import PartitionSpec as P
+
+MESH = pl.DeviceIdType.MESH
 
 decay_rate = 0.95
 epsilon = 1e-06
 CHUNKS = 2
 
 
-def make_body(dp):
+def exchange_kernel(groups, size, src, dst, via_up, via_down, hold, sems):
+    count = groups * size
+    me = lax.axis_index("expert")
+    group, seat = me // size, me % size
+    half = src.shape[2] // 2
+
+    def device(step, shift):
+        return lax.rem(group + step, groups) * size + lax.rem(seat + shift, size)
+
+    def send(source, target, slot, peer):
+        return pltpu.make_async_remote_copy(
+            src_ref=source,
+            dst_ref=target,
+            send_sem=sems.at[0, slot],
+            recv_sem=sems.at[1, slot],
+            device_id={"expert": peer},
+            device_id_type=MESH,
+        )
+
+    barrier = pltpu.get_barrier_semaphore()
+
+    @pl.loop(1, count)
+    def _(step):
+        pl.semaphore_signal(
+            barrier, inc=1, device_id={"expert": lax.rem(me + step, count)}, device_id_type=MESH
+        )
+
+    pl.semaphore_wait(barrier, count - 1)
+
+    own_in = pltpu.make_async_copy(src.at[me], hold, sems.at[0, 0])
+    own_in.start()
+    first, second, slot = [], [], 1
+    for k in range(size):
+        far = device(2, k)
+        up = send(src.at[far, :, pl.ds(0, half)], via_up.at[k], slot, device(1, 0))
+        down = send(src.at[far, :, pl.ds(half, half)], via_down.at[k], slot + 1, device(3, 0))
+        up.start()
+        down.start()
+        first += [up, down]
+        slot += 2
+    for k in range(size):
+        for step in (1, 3, 0):
+            if step == 0 and k == 0:
+                continue
+            copy = send(src.at[device(step, k)], dst.at[me], slot, device(step, k))
+            copy.start()
+            second.append(copy)
+            slot += 1
+    own_in.wait()
+    own_out = pltpu.make_async_copy(hold, dst.at[me], sems.at[0, 0])
+    own_out.start()
+    for k in range(size):
+        first[2 * k].wait_recv()
+        up = send(via_up.at[k], dst.at[device(3, 0), :, pl.ds(0, half)], slot, device(1, k))
+        up.start()
+        first[2 * k + 1].wait_recv()
+        down = send(
+            via_down.at[k], dst.at[device(1, 0), :, pl.ds(half, half)], slot + 1, device(3, k)
+        )
+        down.start()
+        second += [up, down]
+        slot += 2
+    for copy in first:
+        copy.wait_send()
+    for copy in second:
+        copy.wait()
+    own_out.wait()
+
+
+def exchange(blocks, n, identity):
+    count, rows, width = blocks.shape
+    if n % 4 or count != n or width % 256:
+        return lax.all_to_all(blocks, "expert", split_axis=0, concat_axis=0, tiled=True)
+    groups, size = 4, n // 4
+    return pl.pallas_call(
+        functools.partial(exchange_kernel, groups, size),
+        out_shape=jax.ShapeDtypeStruct(blocks.shape, blocks.dtype),
+        in_specs=[pl.BlockSpec(memory_space=pl.ANY)],
+        out_specs=pl.BlockSpec(memory_space=pl.ANY),
+        scratch_shapes=[
+            pltpu.VMEM((size, rows, width // 2), blocks.dtype),
+            pltpu.VMEM((size, rows, width // 2), blocks.dtype),
+            pltpu.VMEM((rows, width), blocks.dtype),
+            pltpu.SemaphoreType.DMA((2, 7 * size)),
+        ],
+        compiler_params=pltpu.CompilerParams(collective_id=identity, has_side_effects=True),
+        cost_estimate=pl.CostEstimate(flops=0, bytes_accessed=250_000_000, transcendentals=0),
+        name=f"exchange_{identity}",
+    )(blocks)
+
+
+def inverse_kernel(lower_ref, out_ref):
+    lower = lower_ref[...]
+    rank = lower.shape[0]
+    row = lax.broadcasted_iota(jnp.int32, lower.shape, 0)
+    col = lax.broadcasted_iota(jnp.int32, lower.shape, 1)
+    diagonal = jnp.sum(jnp.where(row == col, lower, 0.0), axis=1, keepdims=True)
+    result = jnp.where(row == col, 1.0 / diagonal, 0.0)
+    size = 1
+    while size < rank:
+        inside = (row // (2 * size) == col // (2 * size)) & (row // size > col // size)
+        below = jnp.where(inside, lower, 0.0)
+        product = jnp.dot(below, result, precision=lax.Precision.HIGHEST)
+        result = result - jnp.dot(result, product, precision=lax.Precision.HIGHEST)
+        size *= 2
+    out_ref[...] = result
+
+
+def invert(lower):
+    return pl.pallas_call(
+        inverse_kernel,
+        out_shape=jax.ShapeDtypeStruct(lower.shape, lower.dtype),
+        in_specs=[pl.BlockSpec(memory_space=pltpu.VMEM)],
+        out_specs=pl.BlockSpec(memory_space=pltpu.VMEM),
+        name="triangular_inverse",
+    )(lower)
+
+
+def make_body(dp, n):
     def others(value, wire=None):
         sent = value if wire is None else value.astype(wire)
         for step in range(1, dp):
@@ -18,14 +141,13 @@
 
     def body(gradients, momentum, right_factor):
         place = lax.axis_index("dp")
-        experts = gradients.shape[0]
         rows, width = momentum.shape[1], momentum.shape[2]
         depth, rank = right_factor.shape[1], right_factor.shape[2]
         factor = jnp.zeros((dp * depth, rank), right_factor.dtype)
         factor = lax.dynamic_update_slice(factor, right_factor[0], (place * depth, 0))
         for step, block in others(right_factor[0]):
             factor = lax.dynamic_update_slice(factor, block, ((place - step) % dp * depth, 0))
-        arrived = lax.all_to_all(gradients, "expert", split_axis=0, concat_axis=0, tiled=True)
+        arrived = exchange(gradients, n, 1)
         arrived = arrived.reshape(rows, width)
         blended = (
             decay_rate * momentum[0].astype(jnp.float32) + arrived.astype(jnp.float32)
@@ -36,9 +158,7 @@
         for _, block in others(gram):
             gram_matrix = gram_matrix + block
         lower = jnp.linalg.cholesky(gram_matrix)
-        inverse = jax.scipy.linalg.solve_triangular(
-            lower, jnp.eye(rank, dtype=jnp.float32), lower=True
-        )
+        inverse = invert(lower)
         ortho = jnp.dot(left, inverse.T, precision=lax.Precision.HIGHEST).astype(jnp.bfloat16)
         pieces = CHUNKS if width % (128 * CHUNKS) == 0 else 1
         size = width // pieces
@@ -63,13 +183,7 @@
                 ortho, new_factor, (((1,), (1,)), ((), ())), preferred_element_type=jnp.float32
             )
         ).astype(jnp.bfloat16)
-        returned = lax.all_to_all(
-            update.reshape(experts, rows // experts, width),
-            "expert",
-            split_axis=0,
-            concat_axis=0,
-            tiled=True,
-        )
+        returned = exchange(update.reshape(n, rows // n, width), n, 2)
         kept = (
             blended.astype(jnp.float32)
             - (1.0 - decay_rate)
@@ -90,7 +204,7 @@
     in_specs = (P(None, ("dp", "expert"), None), P("expert", "dp", None), P("expert", "dp", None))
     out_specs = (P("expert", "dp", None), P("expert", "dp", None), P(None, ("dp", "expert"), None))
     return jax.shard_map(
-        make_body(mesh.shape["dp"]),
+        make_body(mesh.shape["dp"], mesh.shape["expert"]),
         mesh=mesh,
         in_specs=in_specs,
         out_specs=out_specs,

time: 442 us -> 439 us (level)
  Pallas kernels: 0 us -> 283 us
  waiting for transfers between devices: 318 us -> 71.1 us
  other arithmetic: 62.1 us -> 43.2 us
  starting transfers between devices: 17.3 us -> 3.41 us
    pallas_call x0 -> x3, Pallas kernels: none -> 283 us  [the longest x2 273 us: exchange(): pl.pallas_call(functools.partial(exchange_kernel, groups, size), out_shap...]
    all_to_all x2 -> x0, waiting for transfers between devices: 219 us -> none  [the longest x1 122 us: body(): lax.all_to_all(update.reshape(experts, rows // experts, width), 'expert',...]
    ppermute x4, waiting for transfers between devices: 99.6 us -> 71.1 us  [others(): lax.ppermute(sent, 'dp', [(i, (i + step) % dp) for i in range(dp)])]
    another operation x3 -> x0, other arithmetic: 19.7 us -> none  [body(): jax.scipy.linalg.solve_triangular(lower, jnp.eye(rank, dtype=jnp.float32)...]
    all_to_all x2 -> x0, starting transfers between devices: 13.2 us -> none  [the longest x1 6.67 us: body(): lax.all_to_all(gradients, 'expert', split_axis=0, concat_axis=0, tiled=True)]
  transfers between devices with their start and end apart: 6 -> 4, of which waited for: 6 -> 3; matrix products, arithmetic and copies ran while one was open for 3% -> 2% of each run, Pallas kernels for 0% -> 31%
where the time goes in v2:
time: 439 us; the launch traced here: 437 us
  Pallas kernels  283 us (64%)
  waiting for transfers between devices  71.1 us (16%)
  other arithmetic  43.2 us (10%)
  matrix products  20.1 us (5%)
  local copies, waits for them, and re-layouts  14 us (3%)
    pallas_call x2, Pallas kernels, exchange(): pl.pallas_call(functools.partial(exchange_kernel, groups, size), out_shap...  273 us
    ppermute x4, waiting for transfers between devices, others(): lax.ppermute(sent, 'dp', [(i, (i + step) % dp) for i in range(dp)])  71.1 us
    another operation x6, other arithmetic, body(): lower = jnp.linalg.cholesky(gram_matrix)  34.1 us
    pallas_call x1, Pallas kernels, invert(): pl.pallas_call(inverse_kernel, out_shape=jax.ShapeDtypeStruct(lower.shape...  10.3 us
  transfers between devices with their start and end apart: 4, of which 3 were waited for; matrix products, arithmetic and copies ran while one was open for 2% of the time, Pallas kernels for 31%

profile of v2, /device:TPU:13, one launch (start us, length us, event | category | flops | bytes accessed | tf_op | source)
XLA Modules:
  0.0 436.8 jit_solution(5839089086314004512)
XLA Ops:
  0.6 1.3 collective-permute-start
  1.9 136.0 %exchange_1.1 = bf16[16,32,5888]{2,1,0:T(8,128)(2,1)} custom-call(bf16[16,32,5888]{2,1,0:T(8,128)(2,1)} %src.1), custom_call_target="tpu_custom_call" | custom-call | bytes 250000000 | tf_op jit(solution)/shard_map/exchange_1/pallas_call | solution.py:92
  138.0 1.8 broadcast_in_dim.12
  139.9 1.2 constant_dynamic-update-slice_fusion.2
  141.1 6.2 %fusion = bf16[512,5888]{1,0:T(8,128)(2,1)S(1)} fusion(bf16[1,512,5888]{2,1,0:T(8,128)(2,1)} %param.4, bf16[16,32,5888]{2,1,0:T(8,128)(2,1)} %exchange_1.1), kind=kLoop, calls=%fused_computation.1 | loop fusion | flops 15073280 | bytes 18087936 | tf_op jit(solution)/shard_map/convert_element_type | solution.py:154
  147.4 3.7 constant_dynamic-update-slice_fusion.1
  151.1 3.6 fusion.15
  154.7 1.0 fusion.16
  155.7 0.3 collective-permute-start.1
  156.1 7.9 %collective-permute-done.1 = f32[256,256]{0,1:T(8,128)S(1)} collective-permute-done((f32[256,256]{0,1:T(8,128)S(1)}, f32[256,256]{0,1:T(8,128)S(1)}, u32[]{:S(2)}, u32[]{:S(2)}) %collective-permute-start.1) | collective-permute-done | bytes 262176 | tf_op jit(solution)/shard_map/ppermute | solution.py:140
  164.2 11.7 %cholesky.50 = f32[128,128]{1,0:T(8,128)S(1)} custom-call(f32[128,128]{1,0:T(8,128)S(1)} %cholesky.118), custom_call_target="Cholesky" | custom-call | tf_op jit(solution)/shard_map/jit(cholesky)/cholesky | solution.py:160
  175.9 9.8 %custom-call.11 = f32[1,128,128]{1,2,0:T(8,128)S(1)} custom-call(f32[1,128,128]{2,1,0:T(8,128)S(1)} %get-tuple-element.6), custom_call_target="InvertDiagBlocksLowerTriangular" | custom-call | tf_op jit(solution)/shard_map/jit(cholesky)/cholesky | solution.py:160
  186.2 11.9 %cholesky.105 = f32[128,128]{1,0:T(8,128)S(1)} custom-call(f32[128,128]{1,0:T(8,128)S(1)} %slice_subtract_fusion), custom_call_target="Cholesky" | custom-call | tf_op jit(solution)/shard_map/jit(cholesky)/cholesky | solution.py:160
  198.1 0.6 compare_reduce_fusion
  200.1 0.7 select_select_fusion.lower_ref
  200.8 10.3 %triangular_inverse.1 = f32[256,256]{1,0:T(8,128)} custom-call(f32[256,256]{1,0:T(8,128)} %select_select_fusion.lower_ref), custom_call_target="tpu_custom_call" | custom-call | tf_op jit(solution)/shard_map/triangular_inverse/pallas_call | solution.py:127
  211.1 1.7 convolution_convert_fusion
  212.8 3.0 fusion.13
  215.8 0.3 collective-permute-start.3
  216.2 1.0 fusion.14
  217.2 1.5 collective-permute-start.2
  218.6 31.2 %collective-permute-done.3 = bf16[2944,256]{1,0:T(8,128)(2,1)S(1)} collective-permute-done((bf16[2944,256]{1,0:T(8,128)(2,1)S(1)}, bf16[2944,256]{1,0:T(8,128)(2,1)S(1)}, u32[]{:S(2)}, u32[]{:S(2)}) %collective-permute-start.3) | collective-permute-done | bytes 1507360 | tf_op jit(solution)/shard_map/ppermute | solution.py:140
  249.8 0.3 convert_add_fusion.1
  250.1 32.0 %collective-permute-done.2 = bf16[2944,256]{1,0:T(8,128)(2,1)S(1)} collective-permute-done((bf16[2944,256]{1,0:T(8,128)(2,1)S(1)}, bf16[2944,256]{1,0:T(8,128)(2,1)S(1)}, u32[]{:S(2)}, u32[]{:S(2)}) %collective-permute-start.2) | collective-permute-done | bytes 1507360 | tf_op jit(solution)/shard_map/ppermute | solution.py:140
  282.1 0.3 convert_add_fusion.2
  282.4 5.0 %fusion.1 = bf16[1,512,5888]{2,1,0:T(8,128)(2,1)} fusion(bf16[512,256]{1,0:T(8,128)(2,1)S(1)} %convolution_convert_fusion, bf16[512,5888]{1,0:T(8,128)(2,1)S(1)} %bitcast.37, f32[2944,256]{1,0:T(8,128)S(1)} %convert_add_fusion.1, f32[2944,256]{1,0:T(8,128)S(1)} %convert_add_fusion.2), kind=kOutput, calls=%fused_computation.4 | convolution fusion | flops 1561591808 | bytes 18350080 | tf_op jit(solution)/shard_map/dot_general | solution.py:190
  287.4 0.8 multiply_reduce_fusion
  288.2 0.6 multiply_convert_fusion.1
  288.9 1.2 dynamic-slice_bitcast_fusion
  290.1 4.4 %multiply_convert_fusion = bf16[512,5888]{1,0:T(8,128)(2,1)} fusion(bf16[512,256]{1,0:T(8,128)(2,1)S(1)} %convolution_convert_fusion, bf16[5888,256]{1,0:T(8,128)(2,1)S(1)} %multiply_convert_fusion.1), kind=kOutput, calls=%fused_computation.2 | convolution fusion | flops 1549533184 | bytes 9306112 | tf_op jit(solution)/shard_map/dot_general | solution.py:182
  294.5 136.6 %exchange_2.1 = bf16[16,32,5888]{2,1,0:T(8,128)(2,1)} custom-call(bf16[16,32,5888]{2,1,0:T(8,128)(2,1)} %bitcast.38), custom_call_target="tpu_custom_call" | custom-call | bytes 250000000 | tf_op jit(solution)/shard_map/exchange_2/pallas_call | solution.py:92
  431.1 5.7 %copy.15 = bf16[16,32,5888]{2,1,0:T(8,128)(2,1)} copy(bf16[16,32,5888]{2,1,0:T(8,128)(2,1)} %exchange_2.1) | data formatting | bytes 12058624
  (20 shorter events, 0.9 us)
Async XLA Ops:
  0.6 146.7 %collective-permute-start = (bf16[2944,256]{1,0:T(8,128)(2,1)}, bf16[2944,256]{1,0:T(8,128)(2,1)}, u32[]{:S(2)}, u32[]{:S(2)}) collective-permute-start(bf16[2944,256]{1,0:T(8,128)(2,1)} %bitcast.39), channel_id=1, source_target_pairs={{0,16},{16,0},{1,17},{17,1},{2,18},{18,2},{3,19},{19,3},{4,20},{20... | collective-permute-start | bytes 4521992 | tf_op jit(solution)/shard_map/ppermute | solution.py:140
  138.0 1.9 copy-start.1
  147.4 7.3 %copy-start = (bf16[512,5888]{1,0:T(8,128)(2,1)}, bf16[512,5888]{1,0:T(8,128)(2,1)S(1)}, u32[]{:S(2)}) copy-start(bf16[512,5888]{1,0:T(8,128)(2,1)S(1)} %fusion) | copy-start | bytes 18087940
  155.7 8.2 %collective-permute-start.1 = (f32[256,256]{0,1:T(8,128)S(1)}, f32[256,256]{0,1:T(8,128)S(1)}, u32[]{:S(2)}, u32[]{:S(2)}) collective-permute-start(f32[256,256]{0,1:T(8,128)S(1)} %fusion.16), channel_id=1, source_target_pairs={{0,16},{16,0},{1,17},{17,1},{2,18},{18,2},{3,19},{19,3},{4,20},{20... | collective-permute-start | bytes 786440 | tf_op jit(solution)/shard_map/ppermute | solution.py:140
  211.1 5.0 %slice-start = ((s8[6029312]{0:T(1024)(128)(4,1)}), s8[4194304]{0:T(1024)(128)(4,1)S(1)}, s32[]{:S(2)}) async-start(s8[6029312]{0:T(1024)(128)(4,1)} %bitcast.36), calls=%async_computation | async-start | bytes 8388608
  212.8 3.3 slice-start.1
  215.8 34.0 %collective-permute-start.3 = (bf16[2944,256]{1,0:T(8,128)(2,1)S(1)}, bf16[2944,256]{1,0:T(8,128)(2,1)S(1)}, u32[]{:S(2)}, u32[]{:S(2)}) collective-permute-start(bf16[2944,256]{1,0:T(8,128)(2,1)S(1)} %get-tuple-element.9), channel_id=1, source_target_pairs={{0,16},{16,0},{1,17},{17,1},{2,18},{18,2},{3,19},{19,3},{4,20},{20... | collective-permute-start | bytes 4521992 | tf_op jit(solution)/shard_map/ppermute | solution.py:140
  217.2 65.0 %collective-permute-start.2 = (bf16[2944,256]{1,0:T(8,128)(2,1)S(1)}, bf16[2944,256]{1,0:T(8,128)(2,1)S(1)}, u32[]{:S(2)}, u32[]{:S(2)}) collective-permute-start(bf16[2944,256]{1,0:T(8,128)(2,1)S(1)} %get-tuple-element.11), channel_id=1, source_target_pairs={{0,16},{16,0},{1,17},{17,1},{2,18},{18,2},{3,19},{19,3},{4,20},{20... | collective-permute-start | bytes 4521992 | tf_op jit(solution)/shard_map/ppermute | solution.py:140

commit v3 on v1

--- a/solution.py
+++ b/solution.py
@@ -3,11 +3,76 @@
 import jax
 import jax.numpy as jnp
 from jax import lax
+from jax.experimental import pallas as pl
+from jax.experimental.pallas import tpu as pltpu
 from jax.sharding import PartitionSpec as P
 
 decay_rate = 0.95
 epsilon = 1e-06
 CHUNKS = 2
+
+
+def dot(a, b, contract=(1, 0)):
+    return lax.dot_general(
+        a,
+        b,
+        (((contract[0],), (contract[1],)), ((), ())),
+        precision=lax.Precision.HIGHEST,
+        preferred_element_type=jnp.float32,
+    )
+
+
+def inverted(lower):
+    rank = lower.shape[0]
+    row = lax.broadcasted_iota(jnp.int32, lower.shape, 0)
+    col = lax.broadcasted_iota(jnp.int32, lower.shape, 1)
+    diagonal = jnp.sum(jnp.where(row == col, lower, 0.0), axis=1, keepdims=True)
+    result = jnp.where(row == col, 1.0 / diagonal, 0.0)
+    size = 1
+    while size < rank:
+        inside = (row // (2 * size) == col // (2 * size)) & (row // size > col // size)
+        below = jnp.where(inside, lower, 0.0)
+        result = result - dot(result, dot(below, result))
+        size *= 2
+    return result
+
+
+def panel_kernel(lower, gram, inverse, below, rest):
+    half = lower.shape[0]
+    inverse[...] = inverted(lower[...])
+    below[...] = dot(gram[half:, :half], inverse[...], (1, 1))
+    rest[...] = gram[half:, half:] - dot(below[...], below[...], (1, 1))
+
+
+def join_kernel(lower, first, below, out):
+    half = lower.shape[0]
+    second = inverted(lower[...])
+    out[:half, :half] = first[...]
+    out[:half, half:] = jnp.zeros_like(second)
+    out[half:, :half] = -dot(second, dot(below[...], first[...]))
+    out[half:, half:] = second
+
+
+def cholesky_inverse(gram):
+    half = gram.shape[0] // 2
+    block = jax.ShapeDtypeStruct((half, half), jnp.float32)
+    vmem = pl.BlockSpec(memory_space=pltpu.VMEM)
+    lower = lax.linalg.cholesky(gram[:half, :half], symmetrize_input=False)
+    first, below, rest = pl.pallas_call(
+        panel_kernel,
+        out_shape=(block, block, block),
+        in_specs=[vmem] * 2,
+        out_specs=(vmem, vmem, vmem),
+        name="cholesky_panel",
+    )(lower, gram)
+    lower = lax.linalg.cholesky(rest, symmetrize_input=False)
+    return pl.pallas_call(
+        join_kernel,
+        out_shape=jax.ShapeDtypeStruct(gram.shape, jnp.float32),
+        in_specs=[vmem] * 3,
+        out_specs=vmem,
+        name="cholesky_join",
+    )(lower, first, below)
 
 
 def make_body(dp):
@@ -35,10 +100,7 @@
         gram_matrix = gram
         for _, block in others(gram):
             gram_matrix = gram_matrix + block
-        lower = jnp.linalg.cholesky(gram_matrix)
-        inverse = jax.scipy.linalg.solve_triangular(
-            lower, jnp.eye(rank, dtype=jnp.float32), lower=True
-        )
+        inverse = cholesky_inverse(gram_matrix)
         ortho = jnp.dot(left, inverse.T, precision=lax.Precision.HIGHEST).astype(jnp.bfloat16)
         pieces = CHUNKS if width % (128 * CHUNKS) == 0 else 1
         size = width // pieces

time: 442 us -> 421 us (0.952)
  other arithmetic: 62.1 us -> 36.6 us
  Pallas kernels: 0 us -> 10.4 us
    another operation x9 -> x6, other arithmetic: 53.9 us -> 25.8 us  [the longest x3 13.4 us: cholesky_inverse(): lower = lax.linalg.cholesky(rest, symmetrize_input=False)]
    pallas_call x0 -> x2, Pallas kernels: none -> 10.4 us  [the longest x1 5.41 us: cholesky_inverse(): pl.pallas_call(panel_kernel, out_shape=(block, block, block), in_specs=[v...]
  transfers between devices with their start and end apart: 6 -> 6, of which waited for: 6 -> 6; matrix products, arithmetic and copies ran while one was open for 3% -> 4% of each run, Pallas kernels for 0% -> 0%
where the time goes in v3:
time: 421 us; the launch traced here: 420 us
  waiting for transfers between devices  318 us (76%)
  other arithmetic  36.6 us (9%)
  matrix products  23.6 us (6%)
  starting transfers between devices  17.3 us (4%)
  local copies, waits for them, and re-layouts  13.6 us (3%)
  Pallas kernels  10.4 us (2%)
    all_to_all x1, waiting for transfers between devices, body(): lax.all_to_all(update.reshape(experts, rows // experts, width), 'expert',...  122 us
    ppermute x4, waiting for transfers between devices, others(): lax.ppermute(sent, 'dp', [(i, (i + step) % dp) for i in range(dp)])  99.6 us
    all_to_all x1, waiting for transfers between devices, body(): lax.all_to_all(gradients, 'expert', split_axis=0, concat_axis=0, tiled=True)  96.2 us
    another operation x3, other arithmetic, cholesky_inverse(): lower = lax.linalg.cholesky(rest, symmetrize_input=False)  13.4 us
    another operation x3, other arithmetic, cholesky_inverse(): lower = lax.linalg.cholesky(gram[:half, :half], symmetrize_input=False)  12.5 us
  transfers between devices with their start and end apart: 6, of which 6 were waited for; matrix products, arithmetic and copies ran while one was open for 4% of the time, Pallas kernels for 0%

profile of v3, /device:TPU:13, one launch (start us, length us, event | category | flops | bytes accessed | tf_op | source)
XLA Modules:
  0.0 420.4 jit_solution(15448430435274667587)
XLA Ops:
  0.6 6.7 %all-to-all-start = ((bf16[16,32,5888]{2,1,0:T(8,128)(2,1)}), bf16[16,32,5888]{2,1,0:T(8,128)(2,1)}, u32[]{:S(2)}, u32[]{:S(2)}) async-start(bf16[16,32,5888]{2,1,0:T(8,128)(2,1)} %param.4), calls=%async_computation | async-start | bytes 12058624 | tf_op jit(solution)/shard_map/all_to_all | solution.py:93
  7.3 1.3 collective-permute-start
  8.6 1.8 broadcast_in_dim.10
  10.4 1.2 constant_dynamic-update-slice_fusion.1
  11.6 30.0 %collective-permute-done = bf16[2944,256]{1,0:T(8,128)(2,1)S(1)} collective-permute-done((bf16[2944,256]{1,0:T(8,128)(2,1)S(1)}, bf16[2944,256]{1,0:T(8,128)(2,1)S(1)}, u32[]{:S(2)}, u32[]{:S(2)}) %collective-permute-start) | collective-permute-done | bytes 1507360 | tf_op jit(solution)/shard_map/ppermute | solution.py:82
  41.6 1.2 constant_dynamic-update-slice_fusion
  42.9 96.2 %all-to-all-done = bf16[16,32,5888]{2,1,0:T(8,128)(2,1)} async-done(((bf16[16,32,5888]{2,1,0:T(8,128)(2,1)}), bf16[16,32,5888]{2,1,0:T(8,128)(2,1)}, u32[]{:S(2)}, u32[]{:S(2)}) %all-to-all-start) | async-done | bytes 6029344 | tf_op jit(solution)/shard_map/all_to_all | solution.py:93
  139.1 6.2 %fusion = bf16[512,5888]{1,0:T(8,128)(2,1)S(1)} fusion(bf16[1,512,5888]{2,1,0:T(8,128)(2,1)} %param.5, bf16[16,32,5888]{2,1,0:T(8,128)(2,1)} %all-to-all-done), kind=kLoop, calls=%fused_computation.1 | loop fusion | flops 15073280 | bytes 18087936 | tf_op jit(solution)/shard_map/convert_element_type | solution.py:97
  145.4 5.8 %fusion.13 = f32[512,256]{1,0:T(8,128)S(1)} fusion(bf16[512,5888]{1,0:T(8,128)(2,1)S(1)} %fusion, bf16[5888,256]{1,0:T(8,128)(2,1)} %constant_dynamic-update-slice_fusion), kind=kOutput, calls=%fused_computation.32 | convolution fusion | flops 1543503872 | bytes 9568256 | tf_op jit(solution)/shard_map/dot_general | solution.py:98
  151.1 1.1 fusion.14
  152.2 1.3 collective-permute-start.1
  153.5 6.5 %collective-permute-done.1 = f32[256,256]{1,0:T(8,128)S(1)} collective-permute-done((f32[256,256]{1,0:T(8,128)S(1)}, f32[256,256]{1,0:T(8,128)S(1)}, u32[]{:S(2)}, u32[]{:S(2)}) %collective-permute-start.1) | collective-permute-done | bytes 262176 | tf_op jit(solution)/shard_map/ppermute | solution.py:82
  160.1 11.7 %custom-call.4 = f32[128,128]{1,0:T(8,128)S(1)} custom-call(f32[128,128]{1,0:T(8,128)S(1)} %slice.14), custom_call_target="Cholesky" | custom-call | tf_op jit(solution)/shard_map/cholesky/custom-call.1 | solution.py:60
  172.5 1.3 select_select_fusion.1.lower
  173.9 5.4 %cholesky_panel.1 = (f32[128,128]{1,0:T(8,128)}, f32[128,128]{1,0:T(8,128)}, f32[128,128]{1,0:T(8,128)}) custom-call(f32[128,128]{1,0:T(8,128)} %select_select_fusion.1.lower, f32[256,256]{1,0:T(8,128)} %copy-done.5), custom_call_target="tpu_custom_call" | custom-call | tf_op jit(solution)/shard_map/cholesky_panel/pallas_call | solution.py:61
  179.3 12.7 %custom-call.5 = f32[128,128]{1,0:T(8,128)S(1)} custom-call(f32[128,128]{1,0:T(8,128)} %get-tuple-element.7), custom_call_target="Cholesky" | custom-call | tf_op jit(solution)/shard_map/cholesky/custom-call.1 | solution.py:68
  192.6 1.3 select_select_fusion.lower
  193.9 5.0 %cholesky_join.1 = f32[256,256]{1,0:T(8,128)} custom-call(f32[128,128]{1,0:T(8,128)} %select_select_fusion.lower, f32[128,128]{1,0:T(8,128)} %get-tuple-element.8.first, f32[128,128]{1,0:T(8,128)} %get-tuple-element.9.below), custom_call_target="tpu_custom_call" | custom-call | tf_op jit(solution)/shard_map/cholesky_join/pallas_call | solution.py:69
  198.9 1.7 convolution_convert_fusion
  200.6 3.0 fusion.11
  203.6 1.3 collective-permute-start.3
  204.9 1.0 fusion.12
  206.2 31.0 %collective-permute-done.3 = bf16[2944,256]{1,0:T(8,128)(2,1)S(1)} collective-permute-done((bf16[2944,256]{1,0:T(8,128)(2,1)S(1)}, bf16[2944,256]{1,0:T(8,128)(2,1)S(1)}, u32[]{:S(2)}, u32[]{:S(2)}) %collective-permute-start.3) | collective-permute-done | bytes 1507360 | tf_op jit(solution)/shard_map/ppermute | solution.py:82
  237.6 32.0 %collective-permute-done.2 = bf16[2944,256]{1,0:T(8,128)(2,1)S(1)} collective-permute-done((bf16[2944,256]{1,0:T(8,128)(2,1)S(1)}, bf16[2944,256]{1,0:T(8,128)(2,1)S(1)}, u32[]{:S(2)}, u32[]{:S(2)}) %collective-permute-start.2) | collective-permute-done | bytes 1507360 | tf_op jit(solution)/shard_map/ppermute | solution.py:82
  269.9 0.8 multiply_reduce_fusion
  270.7 0.8 copy-done.1
  272.0 4.4 %multiply_convert_fusion = bf16[512,5888]{1,0:T(8,128)(2,1)} fusion(bf16[512,256]{1,0:T(8,128)(2,1)S(1)} %convolution_convert_fusion, bf16[5888,256]{1,0:T(8,128)(2,1)S(1)} %multiply_convert_fusion.1), kind=kOutput, calls=%fused_computation.2 | convolution fusion | flops 1549533184 | bytes 9306112 | tf_op jit(solution)/shard_map/dot_general | solution.py:124
  276.4 6.5 %all-to-all-start.1 = ((bf16[16,32,5888]{2,1,0:T(8,128)(2,1)}), bf16[16,32,5888]{2,1,0:T(8,128)(2,1)}, u32[]{:S(2)}, u32[]{:S(2)}) async-start(bf16[16,32,5888]{2,1,0:T(8,128)(2,1)} %bitcast.25), calls=%async_computation.1 | async-start | bytes 12058624 | tf_op jit(solution)/shard_map/all_to_all | solution.py:128
  282.9 2.8 dynamic-slice_bitcast_fusion
  285.6 6.7 %fusion.1 = bf16[1,512,5888]{2,1,0:T(8,128)(2,1)} fusion(bf16[512,256]{1,0:T(8,128)(2,1)S(1)} %convolution_convert_fusion, bf16[512,5888]{1,0:T(8,128)(2,1)} %copy-done, f32[2944,256]{1,0:T(8,128)S(1)} %convert_add_fusion.1, f32[2944,256]{1,0:T(8,128)S(1)} %copy-done.2), kind=kOutput, calls=%fused_computation.4 | convolution fusion | flops 1561591808 | bytes 18350080 | tf_op jit(solution)/shard_map/dot_general | solution.py:138
  292.3 122.3 %all-to-all-done.1 = bf16[16,32,5888]{2,1,0:T(8,128)(2,1)} async-done(((bf16[16,32,5888]{2,1,0:T(8,128)(2,1)}), bf16[16,32,5888]{2,1,0:T(8,128)(2,1)}, u32[]{:S(2)}, u32[]{:S(2)}) %all-to-all-start.1) | async-done | bytes 6029344 | tf_op jit(solution)/shard_map/all_to_all | solution.py:128
  414.6 5.7 %copy.9 = bf16[16,32,5888]{2,1,0:T(8,128)(2,1)} copy(bf16[16,32,5888]{2,1,0:T(8,128)(2,1)} %all-to-all-done.1) | data formatting | bytes 12058624
  (27 shorter events, 2.9 us)
Async XLA Ops:
  0.6 6.7 %copy-start.4 = (bf16[1,2944,256]{2,1,0:T(8,128)(2,1)S(1)}, bf16[1,2944,256]{2,1,0:T(8,128)(2,1)}, u32[]{:S(2)}) copy-start(bf16[1,2944,256]{2,1,0:T(8,128)(2,1)} %param.6) | copy-start | bytes 4521988
  0.6 138.5 %all-to-all-start = ((bf16[16,32,5888]{2,1,0:T(8,128)(2,1)}), bf16[16,32,5888]{2,1,0:T(8,128)(2,1)}, u32[]{:S(2)}, u32[]{:S(2)}) async-start(bf16[16,32,5888]{2,1,0:T(8,128)(2,1)} %param.4), calls=%async_computation | async-start | bytes 12058624 | tf_op jit(solution)/shard_map/all_to_all | solution.py:93
  7.3 34.3 %collective-permute-start = (bf16[2944,256]{1,0:T(8,128)(2,1)S(1)}, bf16[2944,256]{1,0:T(8,128)(2,1)S(1)}, u32[]{:S(2)}, u32[]{:S(2)}) collective-permute-start(bf16[2944,256]{1,0:T(8,128)(2,1)S(1)} %bitcast.26), channel_id=1, source_target_pairs={{0,16},{16,0},{1,17},{17,1},{2,18},{18,2},{3,19},{19,3},{4,20},{20... | collective-permute-start | bytes 4521992 | tf_op jit(solution)/shard_map/ppermute | solution.py:82
  145.3 5.8 %copy-start = (bf16[512,5888]{1,0:T(8,128)(2,1)}, bf16[512,5888]{1,0:T(8,128)(2,1)S(1)}, u32[]{:S(2)}) copy-start(bf16[512,5888]{1,0:T(8,128)(2,1)S(1)} %fusion) | copy-start | bytes 18087940
  152.2 7.8 %collective-permute-start.1 = (f32[256,256]{1,0:T(8,128)S(1)}, f32[256,256]{1,0:T(8,128)S(1)}, u32[]{:S(2)}, u32[]{:S(2)}) collective-permute-start(f32[256,256]{1,0:T(8,128)S(1)} %fusion.14), channel_id=1, source_target_pairs={{0,16},{16,0},{1,17},{17,1},{2,18},{18,2},{3,19},{19,3},{4,20},{20... | collective-permute-start | bytes 786440 | tf_op jit(solution)/shard_map/ppermute | solution.py:82
  160.0 13.8 %copy-start.5 = (f32[256,256]{1,0:T(8,128)}, f32[256,256]{1,0:T(8,128)S(1)}, u32[]{:S(2)}) copy-start(f32[256,256]{1,0:T(8,128)S(1)} %add.41.gram) | copy-start | bytes 786436
  198.9 6.0 %slice-start = ((s8[6029312]{0:T(1024)(128)(4,1)}), s8[4194304]{0:T(1024)(128)(4,1)S(1)}, s32[]{:S(2)}) async-start(s8[6029312]{0:T(1024)(128)(4,1)} %bitcast.23), calls=%async_computation.2 | async-start | bytes 8388608
  200.6 4.3 %slice-start.1 = ((s8[6029312]{0:T(1024)(128)(4,1)}), s8[1835008]{0:T(1024)(128)(4,1)S(1)}, s32[]{:S(2)}) async-start(s8[6029312]{0:T(1024)(128)(4,1)} %bitcast.23), calls=%async_computation.3 | async-start | bytes 3670016
  203.6 33.6 %collective-permute-start.3 = (bf16[2944,256]{1,0:T(8,128)(2,1)S(1)}, bf16[2944,256]{1,0:T(8,128)(2,1)S(1)}, u32[]{:S(2)}, u32[]{:S(2)}) collective-permute-start(bf16[2944,256]{1,0:T(8,128)(2,1)S(1)} %get-tuple-element.10), channel_id=1, source_target_pairs={{0,16},{16,0},{1,17},{17,1},{2,18},{18,2},{3,19},{19,3},{4,20},{20... | collective-permute-start | bytes 4521992 | tf_op jit(solution)/shard_map/ppermute | solution.py:82
  205.9 63.7 %collective-permute-start.2 = (bf16[2944,256]{1,0:T(8,128)(2,1)S(1)}, bf16[2944,256]{1,0:T(8,128)(2,1)S(1)}, u32[]{:S(2)}, u32[]{:S(2)}) collective-permute-start(bf16[2944,256]{1,0:T(8,128)(2,1)S(1)} %get-tuple-element.12), channel_id=1, source_target_pairs={{0,16},{16,0},{1,17},{17,1},{2,18},{18,2},{3,19},{19,3},{4,20},{20... | collective-permute-start | bytes 4521992 | tf_op jit(solution)/shard_map/ppermute | solution.py:82
  269.9 1.6 copy-start.1
  272.0 4.4 %copy-start.3 = (bf16[5888,256]{1,0:T(8,128)(2,1)}, bf16[5888,256]{1,0:T(8,128)(2,1)S(1)}, u32[]{:S(2)}) copy-start(bf16[5888,256]{1,0:T(8,128)(2,1)S(1)} %multiply_convert_fusion.1) | copy-start | bytes 9043972
  276.4 138.3 %all-to-all-start.1 = ((bf16[16,32,5888]{2,1,0:T(8,128)(2,1)}), bf16[16,32,5888]{2,1,0:T(8,128)(2,1)}, u32[]{:S(2)}, u32[]{:S(2)}) async-start(bf16[16,32,5888]{2,1,0:T(8,128)(2,1)} %bitcast.25), calls=%async_computation.1 | async-start | bytes 12058624 | tf_op jit(solution)/shard_map/all_to_all | solution.py:128
  282.8 2.8 copy-start.2
